TPU v7x, 16 devices: a whole 2x2x2 slice. The times are simulated.
16 devices in a mesh: data: 16 (over z, y, x, core).
Axes of the slice: x: 2, y: 2, z: 2, core: 2. Of those that a mesh axis runs over, the one named last changes fastest.
Arguments:
- x_in: bfloat16 [65536, 1024], P('data')
- d_out: bfloat16 [65536, 1024], P('data')
- w_stack: bfloat16 [4, 1024, 1024], replicated
- a_old: float32 [4, 1024, 1024], replicated
- s_old: float32 [4, 1024, 1024], replicated
- a_inv: float32 [4, 1024, 1024], replicated
- s_inv: float32 [4, 1024, 1024], replicated
Outputs:
- output 1: float32 [4, 1024, 1024], replicated
- output 2: float32 [4, 1024, 1024], replicated
- output 3: float32 [4, 1024, 1024], replicated
All inputs are finite; a program needn't handle non-finite values.
Results may differ from a plain program's by a relative error of at most 0.00138593.
Values are sent between devices in bfloat16 or wider.
A program may use at most 1 GiB of HBM per device.

v0:
```python
import jax
import jax.numpy as jnp
from jax import lax
from jax.sharding import PartitionSpec as P

RHO = 0.75
ERF_SCALE = 0.7071067811865476
PDF_SCALE = 0.3989422804014327


def gelu_fwd(z_val):
    return 0.5 * z_val * (1.0 + lax.erf(z_val * ERF_SCALE))


def gelu_slope(z_val):
    return 0.5 * (1.0 + lax.erf(z_val * ERF_SCALE)) + z_val * jnp.exp(-0.5 * z_val * z_val) * PDF_SCALE


def tok_gram(lhs_rows, rhs_rows):
    return lax.dot_general(lhs_rows, rhs_rows, (((0,), (0,)), ((), ())), preferred_element_type=jnp.float32)


def times_wt(g_rows, w_mat):
    return lax.dot_general(g_rows, w_mat, (((1,), (1,)), ((), ())), preferred_element_type=jnp.float32)


def precondition(a_inv, w_grad, s_inv):
    left_mul = jnp.einsum("lij,ljk->lik", a_inv, w_grad, precision=lax.Precision.HIGHEST, preferred_element_type=jnp.float32)
    return jnp.einsum("lij,ljk->lik", left_mul, s_inv, precision=lax.Precision.HIGHEST, preferred_element_type=jnp.float32)


def solution(mesh):
    group_size = mesh.shape["data"]

    def local_step(x_loc, dy_loc, w_stack, a_old, s_old, a_inv, s_inv):
        layers = w_stack.shape[0]
        half_rows = x_loc.shape[0] // 2
        tokens = x_loc.shape[0] * group_size
        a_acc = [None] * layers
        s_acc = [None] * layers
        w_acc = [None] * layers
        for micro_idx in range(2):
            lo_row = micro_idx * half_rows
            h_cur = x_loc[lo_row:lo_row + half_rows]
            layer_in = []
            pre_act = []
            for layer_idx in range(layers):
                layer_in.append(h_cur)
                a_part = tok_gram(h_cur, h_cur)
                a_acc[layer_idx] = a_part if micro_idx == 0 else a_acc[layer_idx] + a_part
                z_cur = jnp.dot(h_cur, w_stack[layer_idx], preferred_element_type=jnp.float32).astype(jnp.bfloat16)
                pre_act.append(z_cur)
                if layer_idx < layers - 1:
                    h_cur = gelu_fwd(z_cur.astype(jnp.float32)).astype(jnp.bfloat16)
            g_cur = dy_loc[lo_row:lo_row + half_rows]
            for layer_idx in reversed(range(layers)):
                if layer_idx < layers - 1:
                    g_cur = (dh_cur.astype(jnp.float32) * gelu_slope(pre_act[layer_idx].astype(jnp.float32))).astype(jnp.bfloat16)
                s_part = tok_gram(g_cur, g_cur)
                w_part = tok_gram(layer_in[layer_idx], g_cur)
                s_acc[layer_idx] = s_part if micro_idx == 0 else s_acc[layer_idx] + s_part
                w_acc[layer_idx] = w_part if micro_idx == 0 else w_acc[layer_idx] + w_part
                if layer_idx > 0:
                    dh_cur = times_wt(g_cur, w_stack[layer_idx]).astype(jnp.bfloat16)
        a_sum, s_sum, w_sum = lax.psum((jnp.stack(a_acc), jnp.stack(s_acc), jnp.stack(w_acc)), "data")
        a_new = RHO * a_old + (1.0 - RHO) * (a_sum / tokens)
        s_new = RHO * s_old + (1.0 - RHO) * (s_sum / tokens)
        u_stack = precondition(a_inv, w_sum / tokens, s_inv)
        return u_stack, a_new, s_new

    row_spec = P("data", None)
    full_spec = P()
    return jax.shard_map(local_step, mesh=mesh, in_specs=(row_spec, row_spec, full_spec, full_spec, full_spec, full_spec, full_spec), out_specs=(full_spec, full_spec, full_spec), check_vma=False)
```

profile of v0, /device:TPU:0, one launch (start us, length us, event | category | flops | bytes accessed | tf_op | source)
XLA Modules:
  0.0 949.5 jit_solution(1012239346645779024)
XLA Ops:
  7.2 0.0 all-reduce.3.cloned.1.call-start
  7.2 10.2 %fusion.57 = f32[1024,1024]{1,0:T(8,128)} fusion(bf16[4096,1024]{1,0:T(8,128)(2,1)} %param.7), kind=kOutput, calls=%fused_computation.110 | convolution fusion | flops 4294967296 | bytes 8388608 | tf_op jit(solution)/shard_map/dot_general | solution.py:20
  17.4 6.6 fusion.62
  24.1 8.2 fusion.30
  32.2 9.1 fusion.39
  41.3 2.0 copy-done
  43.3 6.3 convolution_convert_fusion
  49.6 10.4 %fusion.53 = bf16[2048,1024]{1,0:T(8,128)(2,1)S(1)} fusion(bf16[2048,1024]{1,0:T(8,128)(2,1)S(1)} %convolution_convert_fusion, bf16[4096,1024]{1,0:T(8,128)(2,1)S(1)} %copy-done.11, bf16[4,1024,1024]{2,1,0:T(8,128)(2,1)} %param.9), kind=kOutput, calls=%fused_computation.88 | convolution fusion | flops 4322230272 | bytes 14680064 | tf_op jit(solution)/shard_map/dot_general | solution.py:24
  60.0 6.8 fusion.64
  66.8 8.2 fusion.3
  75.0 1.9 copy-done.15
  76.9 4.7 fusion.122
  81.7 9.0 fusion.12
  90.7 2.0 copy-done.13
  92.6 7.6 convolution_convert_fusion.3
  100.3 10.6 %fusion.26 = bf16[2048,1024]{1,0:T(8,128)(2,1)} fusion(bf16[2048,1024]{1,0:T(8,128)(2,1)} %convolution_convert_fusion.3, bf16[4096,1024]{1,0:T(8,128)(2,1)S(1)} %copy-done.11, bf16[4,1024,1024]{2,1,0:T(8,128)(2,1)} %param.9), kind=kOutput, calls=%fused_computation.61 | convolution fusion | flops 4322230272 | bytes 14680064 | tf_op jit(solution)/shard_map/dot_general | solution.py:24
  110.9 9.7 %fusion.19 = bf16[2048,1024]{1,0:T(8,128)(2,1)S(1)} fusion(bf16[2048,1024]{1,0:T(8,128)(2,1)} %get-tuple-element.13, bf16[2048,1024]{1,0:T(8,128)(2,1)} %fusion.26, bf16[4,1024,1024]{2,1,0:T(8,128)(2,1)} %param.9), kind=kOutput, calls=%fused_computation.54 | convolution fusion | flops 4322230272 | bytes 14680064 | tf_op jit(solution)/shard_map/dot_general | solution.py:24
  120.7 9.8 %fusion.119 = f32[1024,1024]{0,1:T(8,128)} fusion(bf16[2048,1024]{1,0:T(8,128)(2,1)} %copy-done.15, bf16[2048,1024]{1,0:T(8,128)(2,1)S(1)} %fusion.19), kind=kOutput, calls=%fused_computation.156 | convolution fusion | flops 4294967296 | bytes 12582912 | tf_op jit(solution)/shard_map/dot_general | solution.py:20
  130.5 6.5 fusion.125
  137.0 11.1 %fusion.112 = f32[1024,1024]{1,0:T(8,128)} fusion(bf16[2048,1024]{1,0:T(8,128)(2,1)} %convolution_convert_fusion.3), kind=kOutput, calls=%fused_computation.155 | convolution fusion | flops 4307550208 | bytes 8388608 | tf_op jit(solution)/shard_map/dot_general | solution.py:20
  148.1 10.1 %fusion.126 = f32[1024,1024]{1,0:T(8,128)} fusion(bf16[2048,1024]{1,0:T(8,128)(2,1)} %fusion.26), kind=kOutput, calls=%fused_computation.163 | convolution fusion | flops 4294967296 | bytes 8388608 | tf_op jit(solution)/shard_map/dot_general | solution.py:20
  158.2 8.4 fusion.120
  166.6 6.3 fusion.123
  172.8 7.8 add_bitcast_fusion.7
  180.6 7.8 add_bitcast_fusion
  188.4 9.9 %fusion.46 = bf16[2048,1024]{1,0:T(8,128)(2,1)S(1)} fusion(bf16[2048,1024]{1,0:T(8,128)(2,1)} %get-tuple-element.9, bf16[2048,1024]{1,0:T(8,128)(2,1)S(1)} %fusion.53, bf16[4,1024,1024]{2,1,0:T(8,128)(2,1)} %param.9), kind=kOutput, calls=%fused_computation.81 | convolution fusion | flops 4322230272 | bytes 14680064 | tf_op jit(solution)/shard_map/dot_general | solution.py:24
  198.3 9.3 fusion.37
  207.7 8.5 fusion.59
  216.2 4.6 add_bitcast_fusion.6
  220.8 10.2 %add_bitcast_fusion.8 = f32[1,1024,1024]{1,2,0:T(8,128)} fusion(f32[1024,1024]{0,1:T(8,128)} %fusion.64, bf16[4096,1024]{1,0:T(8,128)(2,1)} %param.8, bf16[2048,1024]{1,0:T(8,128)(2,1)} %convolution_convert_fusion.3), kind=kOutput, calls=%fused_computation.100 | convolution fusion | flops 4308598784 | bytes 16777216 | tf_op jit(solution)/shard_map/dot_general | solution.py:20
  231.0 9.8 %fusion.10 = bf16[2048,1024]{1,0:T(8,128)(2,1)S(1)} fusion(bf16[2048,1024]{1,0:T(8,128)(2,1)} %get-tuple-element.11, bf16[2048,1024]{1,0:T(8,128)(2,1)} %copy-done.12, bf16[4,1024,1024]{2,1,0:T(8,128)(2,1)} %param.9), kind=kOutput, calls=%fused_computation.45 | convolution fusion | flops 4322230272 | bytes 14680064 | tf_op jit(solution)/shard_map/dot_general | solution.py:24
  240.8 2.0 copy-done.6
  242.8 6.1 fusion.124
  249.0 7.6 add_bitcast_fusion.11
  256.6 7.7 add_bitcast_fusion.3
  264.3 8.0 add_bitcast_fusion.10
  272.2 6.5 add_bitcast_fusion.2
  278.8 11.4 %add_bitcast_fusion.4 = f32[1,1024,1024]{2,1,0:T(8,128)} fusion(f32[1024,1024]{1,0:T(8,128)S(1)} %copy-done.16, bf16[2048,1024]{1,0:T(8,128)(2,1)} %copy-done.18), kind=kOutput, calls=%fused_computation.96 | convolution fusion | flops 4308598784 | bytes 12582912 | tf_op jit(solution)/shard_map/dot_general | solution.py:20
  290.1 6.4 add_bitcast_fusion.5
  296.5 7.8 add_bitcast_fusion.9
  304.3 6.5 add_bitcast_fusion.1
  310.9 6.6 pad_maximum_fusion.2
  317.5 12.0 %pad_maximum_fusion = f32[4,1024,1024]{1,2,0:T(8,128)} fusion(f32[1,1024,1024]{1,2,0:T(8,128)S(1)} %copy-done.9, f32[1,1024,1024]{1,2,0:T(8,128)} %add_bitcast_fusion.9, f32[1,1024,1024]{1,2,0:T(8,128)} %add_bitcast_fusion.10, f32[1,1024,1024]{1,2,0:T(8,128)S(1)} %add_bitcast_fusion.11), kind=kLoop, calls=%fused_computation | loop fusion | flops 12582912 | bytes 33554432 | tf_op jit(solution)/shard_map/stack | solution.py:65
  329.4 6.3 pad_maximum_fusion.1
  335.8 455.9 %all-reduce.3.cloned.1.call-done = (f32[4,1024,1024]{1,2,0:T(8,128)}, f32[4,1024,1024]{2,1,0:T(8,128)}, f32[4,1024,1024]{2,1,0:T(8,128)}) async-done(((f32[4,1024,1024]{1,2,0:T(8,128)}, f32[4,1024,1024]{2,1,0:T(8,128)}, f32[4,1024,1024]{2,1,0:T(8,128)}), (f32[4,1024,1024]{1,2,0:T(8,128)}, f32[4,1024,1024]{2,1,0:T(8,128)}, f32[4,1024,1024]{2,1,0:T(8,128)})) %all-reduce.3.cloned.1.call-update) | async-done | bytes 50331664 | tf_op jit(solution)/shard_map/psum | solution.py:65
  791.7 58.5 %fusion = f32[4,1024,1024]{1,2,0:T(8,128)S(1)} fusion(f32[4,1024,1024]{2,1,0:T(8,128)} %param.12, f32[4,1024,1024]{1,2,0:T(8,128)} %get-tuple-element.3), kind=kOutput, calls=%fused_computation.5 | convolution fusion | flops 51543801856 | bytes 50331648 | tf_op jit(solution)/shard_map/lij,ljk->lik/dot_general | solution.py:28
  850.2 58.3 %fusion.121 = f32[4,1024,1024]{2,1,0:T(8,128)} fusion(f32[4,1024,1024]{1,2,0:T(8,128)S(1)} %fusion, f32[4,1024,1024]{2,1,0:T(8,128)} %param.13), kind=kOutput, calls=%fused_computation.158 | convolution fusion | flops 51539607552 | bytes 50331648 | tf_op jit(solution)/shard_map/lij,ljk->lik/dot_general | solution.py:29
  908.5 34.0 %multiply_add_fusion = (f32[4,1024,1024]{2,1,0:T(8,128)}, f32[4,1024,1024]{2,1,0:T(8,128)}) fusion(f32[4,1024,1024]{2,1,0:T(8,128)} %get-tuple-element.5, f32[4,1024,1024]{2,1,0:T(8,128)} %param.11, f32[4,1024,1024]{2,1,0:T(8,128)} %get-tuple-element.4, f32[4,1024,1024]{2,1,0:T(8,128)} %param.10), kind=kLoop, calls=%fused_computation.3 | loop fusion | flops 25165824 | bytes 100663296 | tf_op jit(solution)/shard_map/add | solution.py:67
  (40 shorter events, 0.1 us)
Async XLA Ops:
  7.2 784.5 %all-reduce.3.cloned.1.call-start = ((), (), s32[]{:S(2)}) async-start(), calls=%async_computation | async-start | bytes 100663296 | tf_op jit(solution)/shard_map/psum | solution.py:65
  7.2 10.2 %copy-start.11 = (bf16[4096,1024]{1,0:T(8,128)(2,1)S(1)}, bf16[4096,1024]{1,0:T(8,128)(2,1)}, u32[]{:S(2)}) copy-start(bf16[4096,1024]{1,0:T(8,128)(2,1)} %param.8) | copy-start | bytes 25165828
  7.2 16.8 %slice-start = ((s8[8388608]{0:T(1024)(128)(4,1)}), s8[4194304]{0:T(1024)(128)(4,1)S(1)}, s32[]{:S(2)}) async-start(s8[8388608]{0:T(1024)(128)(4,1)} %bitcast.104), calls=%async_computation.1 | async-start | bytes 8388608
  17.4 6.7 slice-start.1
  32.2 9.1 copy-start.2
  41.3 2.0 copy-start
  49.6 10.4 %copy-start.18 = (bf16[2048,1024]{1,0:T(8,128)(2,1)}, bf16[2048,1024]{1,0:T(8,128)(2,1)S(1)}, u32[]{:S(2)}) copy-start(bf16[2048,1024]{1,0:T(8,128)(2,1)S(1)} %convolution_convert_fusion) | copy-start | bytes 12582916
  75.0 2.0 copy-start.15
  90.7 2.0 copy-start.13
  120.6 9.8 %copy-start.12 = (bf16[2048,1024]{1,0:T(8,128)(2,1)}, bf16[2048,1024]{1,0:T(8,128)(2,1)S(1)}, u32[]{:S(2)}) copy-start(bf16[2048,1024]{1,0:T(8,128)(2,1)S(1)} %fusion.19) | copy-start | bytes 12582916
  148.1 10.1 %copy-start.14 = (bf16[2048,1024]{1,0:T(8,128)(2,1)S(1)}, bf16[2048,1024]{1,0:T(8,128)(2,1)}, u32[]{:S(2)}) copy-start(bf16[2048,1024]{1,0:T(8,128)(2,1)} %copy-done.13) | copy-start | bytes 12582916
  188.4 9.9 %copy-start.17 = (bf16[2048,1024]{1,0:T(8,128)(2,1)S(1)}, bf16[2048,1024]{1,0:T(8,128)(2,1)}, u32[]{:S(2)}) copy-start(bf16[2048,1024]{1,0:T(8,128)(2,1)} %get-tuple-element.7) | copy-start | bytes 12582916
  207.7 8.5 copy-start.3
  240.8 2.0 copy-start.6
  242.8 6.1 copy-start.5
  272.2 6.5 copy-start.16
  278.8 11.4 %copy-start.1 = (bf16[2048,1024]{1,0:T(8,128)(2,1)S(1)}, bf16[2048,1024]{1,0:T(8,128)(2,1)}, u32[]{:S(2)}) copy-start(bf16[2048,1024]{1,0:T(8,128)(2,1)} %copy-done) | copy-start | bytes 12582916
  304.3 6.5 copy-start.4
  304.3 6.5 copy-start.8
  310.8 6.6 copy-start.9
  317.5 12.0 %copy-start.7 = (f32[1,1024,1024]{2,1,0:T(8,128)S(1)}, f32[1,1024,1024]{2,1,0:T(8,128)}, u32[]{:S(2)}) copy-start(f32[1,1024,1024]{2,1,0:T(8,128)} %add_bitcast_fusion.7) | copy-start | bytes 12582916
  317.5 12.0 %copy-start.10 = (f32[1,1024,1024]{2,1,0:T(8,128)S(1)}, f32[1,1024,1024]{2,1,0:T(8,128)}, u32[]{:S(2)}) copy-start(f32[1,1024,1024]{2,1,0:T(8,128)} %add_bitcast_fusion.4) | copy-start | bytes 12582916
Sparse Core Ops, SparseCore 0:
  335.9 455.7 all-reduce.2
where the time goes:
time: 954 us; the launch traced here: 950 us
  waiting for transfers between devices  456 us (48%)
  matrix products  412 us (43%)
  other arithmetic  58.9 us (6%)
  between operations  14.5 us (2%)
    psum x1, waiting for transfers between devices, local_step(): lax.psum((jnp.stack(a_acc), jnp.stack(s_acc), jnp.stack(w_acc)), 'data')  456 us
    dot_general x24, matrix products, tok_gram(): lax.dot_general(lhs_rows, rhs_rows, (((0,), (0,)), ((), ())), preferred_e...  187 us
    dot_general x6, matrix products, times_wt(): lax.dot_general(g_rows, w_mat, (((1,), (1,)), ((), ())), preferred_elemen...  59.7 us
    dot_general x1, matrix products, precondition(): jnp.einsum('lij,ljk->lik', a_inv, w_grad, precision=lax.Precision.HIGHEST...  58.5 us
    dot_general x1, matrix products, precondition(): jnp.einsum('lij,ljk->lik', left_mul, s_inv, precision=lax.Precision.HIGHE...  58.3 us
    dot_general x6, matrix products, local_step(): jnp.dot(h_cur, w_stack[layer_idx], preferred_element_type=jnp.float32)  48.4 us
    add x1, other arithmetic, local_step(): s_new = RHO * s_old + (1.0 - RHO) * (s_sum / tokens)  34 us
  transfers between devices with their start and end apart: 1, of which 1 were waited for; matrix products, arithmetic and copies ran while one was open for 0% of the time, Pallas kernels for 0%

commit v1 on v0

v1 whole, which is shorter than its diff:
```python
import jax
import jax.numpy as jnp
from jax import lax
from jax.sharding import PartitionSpec as P

RHO = 0.75
ERF_SCALE = 0.7071067811865476
PDF_SCALE = 0.3989422804014327
BLK = 128


def tok_gram(lhs_rows, rhs_rows):
    return lax.dot_general(lhs_rows, rhs_rows, (((0,), (0,)), ((), ())), preferred_element_type=jnp.float32)


def times_wt(g_rows, w_mat):
    return lax.dot_general(g_rows, w_mat, (((1,), (1,)), ((), ())), preferred_element_type=jnp.float32)


def gelu_pair(z_val):
    cdf = 0.5 * (1.0 + lax.erf(z_val * ERF_SCALE))
    return z_val * cdf, cdf + z_val * jnp.exp(-0.5 * z_val * z_val) * PDF_SCALE


def pack_halves(top, bot, row0):
    rows, d = top.shape
    half = bot.shape[1]
    r_blk = (row0 + lax.broadcasted_iota(jnp.int32, (rows, d + BLK), 0)) // BLK
    pos = lax.broadcasted_iota(jnp.int32, (rows, d + BLK), 1)
    return jnp.where(pos < BLK * (r_blk + 1), jnp.pad(bot, ((0, 0), (0, d + BLK - half))), jnp.pad(top, ((0, 0), (BLK, 0))))


def sym_gram_packed(rows):
    half = rows.shape[1] // 2
    top = tok_gram(rows[:, :half], rows)
    bot = tok_gram(rows[:, half:], rows[:, half:])
    return pack_halves(top, bot, 0)


def mirror(sq):
    n = sq.shape[0]
    r_blk = lax.broadcasted_iota(jnp.int32, (n, n), 0) // BLK
    c_blk = lax.broadcasted_iota(jnp.int32, (n, n), 1) // BLK
    return r_blk, c_blk


def unpack(packed):
    half = packed.shape[0]
    r_blk = lax.broadcasted_iota(jnp.int32, (half, half), 0) // BLK
    c_blk = lax.broadcasted_iota(jnp.int32, (half, half), 1) // BLK
    tl = packed[:, BLK:BLK + half]
    tr = packed[:, BLK + half:]
    br = packed[:, :half]
    tl = jnp.where(c_blk >= r_blk, tl, tl.T)
    br = jnp.where(c_blk <= r_blk, br, br.T)
    return jnp.concatenate([jnp.concatenate([tl, tr], 1), jnp.concatenate([tr.T, br], 1)], 0)


def hi_dot(lhs, rhs, dims):
    return lax.dot_general(lhs, rhs, (dims, ((), ())), precision=lax.Precision.HIGHEST, preferred_element_type=jnp.float32)


def solution(mesh):
    group_size = mesh.shape["data"]

    def local_step(x_loc, dy_loc, w_stack, a_old, s_old, a_inv, s_inv):
        layers, d = w_stack.shape[0], w_stack.shape[1]
        half = d // 2
        tokens = x_loc.shape[0] * group_size
        me = lax.axis_index("data")
        sh = half // group_size

        def scatter(mats):
            return lax.psum_scatter(jnp.concatenate(mats, 1), "data", scatter_dimension=0, tiled=True)

        def gather(mats):
            return lax.all_gather(jnp.concatenate(mats, 1), "data", axis=0, tiled=True)

        def old_shard(old):
            top = lax.dynamic_slice(old, (me * sh, 0), (sh, d))
            bot = lax.dynamic_slice(old, (half + me * sh, half), (sh, half))
            return pack_halves(top, bot, me * sh)

        pw = d + BLK
        a_fac = [None] * layers
        s_fac = [None] * layers
        w_fac = [None] * layers

        def blend(old, red):
            return RHO * old_shard(old) + (1.0 - RHO) * (red / tokens)

        h_in = [x_loc]
        slope = []
        a_pk = [sym_gram_packed(x_loc)]
        s_pk = [None] * layers
        s_pk[layers - 1] = sym_gram_packed(dy_loc)
        red0 = scatter([a_pk[0], s_pk[layers - 1]])
        for l in range(layers - 1):
            z_cur = jnp.dot(h_in[l], w_stack[l], preferred_element_type=jnp.float32).astype(jnp.bfloat16)
            h_nxt, sl = gelu_pair(z_cur.astype(jnp.float32))
            h_in.append(h_nxt.astype(jnp.bfloat16))
            slope.append(sl)
            a_pk.append(sym_gram_packed(h_in[l + 1]))
        red1 = scatter(a_pk[1:])
        new0 = [blend(a_old[0], red0[:, :pw]), blend(s_old[layers - 1], red0[:, pw:])]
        new1 = [blend(a_old[l], red1[:, (l - 1) * pw:l * pw]) for l in range(1, layers)]
        a_all = gather(new0[:1] + new1 + new0[1:])
        a_new = [unpack(a_all[:, l * pw:(l + 1) * pw]) for l in range(layers)]
        s_new = [None] * layers
        s_new[layers - 1] = unpack(a_all[:, layers * pw:])

        g_cur = dy_loc
        t_loc = [None] * layers
        s_sh = [None] * layers
        for l in reversed(range(layers)):
            if l < layers - 1:
                dh = times_wt(g_cur, w_stack[l + 1]).astype(jnp.bfloat16)
                g_cur = (dh.astype(jnp.float32) * slope[l]).astype(jnp.bfloat16)
            dwt = tok_gram(g_cur, h_in[l])
            mats = [dwt[:half], dwt[half:]]
            if l < layers - 1:
                mats.append(sym_gram_packed(g_cur))
            red = scatter(mats)
            if l < layers - 1:
                s_sh[l] = blend(s_old[l], red[:, 2 * d:])
            rows = jnp.concatenate([red[:, :d], red[:, d:2 * d]], 0) / tokens
            t_loc[l] = hi_dot(a_inv[l], rows, ((1,), (1,)))
        s_all = gather(s_sh[:layers - 1])
        for l in range(layers - 1):
            s_new[l] = unpack(s_all[:, l * pw:(l + 1) * pw])

        t_st = jnp.stack(t_loc, 0)
        q = d // group_size
        t_x = lax.all_to_all(t_st.reshape(layers, group_size, q, 2, sh), "data", split_axis=1, concat_axis=1, tiled=True)
        t_rows = t_x.transpose(0, 2, 3, 1, 4).reshape(layers, q, d)
        u_loc = jnp.stack([hi_dot(t_rows[l], s_inv[l], ((1,), (0,))) for l in range(layers)], 0)
        u_stack = lax.all_gather(u_loc, "data", axis=1, tiled=True)
        return u_stack, jnp.stack(a_new), jnp.stack(s_new)

    row_spec = P("data", None)
    full_spec = P()
    return jax.shard_map(local_step, mesh=mesh, in_specs=(row_spec, row_spec, full_spec, full_spec, full_spec, full_spec, full_spec), out_specs=(full_spec, full_spec, full_spec), check_vma=False)
```

time: 954 us -> 913 us (0.957)
  local copies, waits for them, and re-layouts: 7.95 us -> 181 us
  waiting for transfers between devices: 456 us -> 285 us
  matrix products: 412 us -> 286 us
  other arithmetic: 58.9 us -> 110 us
  blocking collectives: 0 us -> 24.1 us
    psum x1 -> x0, waiting for transfers between devices: 456 us -> none  [local_step(): lax.psum((jnp.stack(a_acc), jnp.stack(s_acc), jnp.stack(w_acc)), 'data')]
    reduce_scatter x0 -> x5, waiting for transfers between devices: none -> 227 us  [scatter(): lax.psum_scatter(jnp.concatenate(mats, 1), 'data', scatter_dimension=0, t...]
    unnamed x42 -> x148, local copies, waits for them, and re-layouts: 7.95 us -> 104 us
    dot_general x8 -> x11, matrix products: 165 us -> 88.9 us  [the longest x8 46.5 us: hi_dot(): lax.dot_general(lhs, rhs, (dims, ((), ())), precision=lax.Precision.HIGHE...]
    unnamed x1 -> x10, waiting for transfers between devices: 0.02 us -> 57.5 us
    slice x0 -> x21, local copies, waits for them, and re-layouts: none -> 47.5 us  [the longest x5 23.8 us: unpack(): tl = packed[:, BLK:BLK + half]]
    dot_general x24 -> x20, matrix products: 187 us -> 148 us  [tok_gram(): lax.dot_general(lhs_rows, rhs_rows, (((0,), (0,)), ((), ())), preferred_e...]
    select_n x0 -> x4, other arithmetic: none -> 37.1 us  [the longest x3 24.2 us: unpack(): tl = jnp.where(c_blk >= r_blk, tl, tl.T)]
  transfers between devices with their start and end apart: 1 -> 9, of which waited for: 1 -> 4; matrix products, arithmetic and copies ran while one was open for 0% -> 38% of each run, Pallas kernels for 0% -> 0%
where the time goes in v1:
time: 913 us; the launch traced here: 902 us
  matrix products  286 us (31%)
  waiting for transfers between devices  285 us (31%)
  local copies, waits for them, and re-layouts  181 us (20%)
  other arithmetic  110 us (12%)
  blocking collectives  24.1 us (3%)
  between operations  14.9 us (2%)
    reduce_scatter x5, waiting for transfers between devices, scatter(): lax.psum_scatter(jnp.concatenate(mats, 1), 'data', scatter_dimension=0, t...  227 us
    dot_general x20, matrix products, tok_gram(): lax.dot_general(lhs_rows, rhs_rows, (((0,), (0,)), ((), ())), preferred_e...  148 us
    unnamed x148, local copies, waits for them, and re-layouts  104 us
    unnamed x10, waiting for transfers between devices  57.5 us
    dot_general x3, matrix products, times_wt(): lax.dot_general(g_rows, w_mat, (((1,), (1,)), ((), ())), preferred_elemen...  49.4 us
    dot_general x8, matrix products, hi_dot(): lax.dot_general(lhs, rhs, (dims, ((), ())), precision=lax.Precision.HIGHE...  46.5 us
    dot_general x3, matrix products, local_step(): jnp.dot(h_in[l], w_stack[l], preferred_element_type=jnp.float32)  42.5 us
    another operation x10, other arithmetic, local_step(): return (u_stack, jnp.stack(a_new), jnp.stack(s_new))  34.8 us
  transfers between devices with their start and end apart: 9, of which 4 were waited for; matrix products, arithmetic and copies ran while one was open for 38% of the time, Pallas kernels for 0%

profile of v1, /device:TPU:0, one launch (start us, length us, event | category | flops | bytes accessed | tf_op | source)
XLA Modules:
  0.0 901.9 jit_solution(4610513241268269590)
XLA Ops:
  8.4 6.9 fusion.73
  15.3 5.9 fusion.71
  21.2 7.0 fusion.69
  28.2 11.1 %fusion.67 = f32[512,1024]{0,1:T(8,128)} fusion(bf16[4096,1024]{1,0:T(8,128)(2,1)} %param.8), kind=kOutput, calls=%fused_computation.101 | convolution fusion | flops 4294967296 | bytes 14680064 | tf_op jit(solution)/shard_map/dot_general | solution.py:13
  39.3 13.3 %fusion.3 = (bf16[4096,1024]{1,0:T(8,128)(2,1)}, bf16[4096,1024]{1,0:T(8,128)(2,1)}) fusion(bf16[4096,1024]{1,0:T(8,128)(2,1)S(1)} %copy-done.40, bf16[4,1024,1024]{2,1,0:T(8,128)(2,1)S(1)} %bitcast.233), kind=kOutput, calls=%fused_computation.18 | convolution fusion | flops 8619294720 | bytes 27262976 | tf_op jit(solution)/shard_map/dot_general | solution.py:99
  52.6 7.0 fusion.37
  59.5 5.9 fusion.35
  65.4 13.7 %fusion.12 = (bf16[4096,1024]{1,0:T(8,128)(2,1)S(1)}, bf16[4096,1024]{1,0:T(8,128)(2,1)}) fusion(bf16[4096,1024]{1,0:T(8,128)(2,1)} %get-tuple-element.95, bf16[4,1024,1024]{2,1,0:T(8,128)(2,1)S(1)} %bitcast.233), kind=kOutput, calls=%fused_computation.27 | convolution fusion | flops 8619294720 | bytes 27262976 | tf_op jit(solution)/shard_map/dot_general | solution.py:99
  82.7 5.8 fusion.31
  88.5 15.5 %fusion.26 = (bf16[4096,1024]{1,0:T(8,128)(2,1)}, bf16[4096,1024]{1,0:T(8,128)(2,1)}) fusion(bf16[4096,1024]{1,0:T(8,128)(2,1)} %copy-done.42, bf16[4,1024,1024]{2,1,0:T(8,128)(2,1)S(1)} %bitcast.233), kind=kOutput, calls=%fused_computation.41 | convolution fusion | flops 8619294720 | bytes 27262976 | tf_op jit(solution)/shard_map/dot_general | solution.py:99
  104.1 16.0 %fusion.25 = bf16[4096,1024]{1,0:T(8,128)(2,1)S(1)} fusion(bf16[4096,1024]{1,0:T(8,128)(2,1)} %get-tuple-element.100, bf16[4096,1024]{1,0:T(8,128)(2,1)S(1)} %bitcast.235, bf16[4,1024,1024]{2,1,0:T(8,128)(2,1)S(1)} %bitcast.233), kind=kOutput, calls=%fused_computation.40 | convolution fusion | flops 8644460544 | bytes 27262976 | tf_op jit(solution)/shard_map/dot_general | solution.py:17
  120.2 17.3 %fusion.17 = bf16[4096,1024]{1,0:T(8,128)(2,1)S(1)} fusion(bf16[4096,1024]{1,0:T(8,128)(2,1)} %get-tuple-element.98, bf16[4096,1024]{1,0:T(8,128)(2,1)S(1)} %fusion.25, bf16[4,1024,1024]{2,1,0:T(8,128)(2,1)S(1)} %bitcast.233), kind=kOutput, calls=%fused_computation.32 | convolution fusion | flops 8644460544 | bytes 27262976 | tf_op jit(solution)/shard_map/dot_general | solution.py:17
  144.3 10.6 %fusion.43 = f32[512,1024]{0,1:T(8,128)} fusion(bf16[4096,1024]{1,0:T(8,128)(2,1)} %copy-done.46), kind=kOutput, calls=%fused_computation.68 | convolution fusion | flops 4294967296 | bytes 14680064 | tf_op jit(solution)/shard_map/dot_general | solution.py:13
  158.3 6.1 fusion.39
  164.4 16.1 %fusion.8 = bf16[4096,1024]{1,0:T(8,128)(2,1)S(1)} fusion(bf16[4096,1024]{1,0:T(8,128)(2,1)} %get-tuple-element.96, bf16[4096,1024]{1,0:T(8,128)(2,1)} %copy-done.46, bf16[4,1024,1024]{2,1,0:T(8,128)(2,1)S(1)} %bitcast.233), kind=kOutput, calls=%fused_computation.23 | convolution fusion | flops 8644460544 | bytes 27262976 | tf_op jit(solution)/shard_map/dot_general | solution.py:17
  185.1 5.9 fusion.47
  194.4 6.3 fusion.27
  200.7 12.9 %pad_select_fusion.2 = (f32[512,1152]{0,1:T(8,128)}, f32[512,1152]{0,1:T(8,128)}, f32[512,1152]{0,1:T(8,128)}, f32[512,1152]{0,1:T(8,128)S(1)}, f32[512,1152]{0,...) fusion(f32[512,1024]{0,1:T(8,128)} %fusion.35, f32[512,512]{0,1:T(8,128)} %fusion.37, ...), kind=kLoop, calls=%fused_computation.119 | loop fusion | flops 7077888 | bytes 44044800 | tf_op jit(solution)/shard_map/jit(_where)/select_n | solution.py:30
  216.3 6.1 copy.384
  222.4 5.1 pad_maximum_fusion.2
  227.5 8.0 copy.386
  235.6 13.3 %fusion.170 = f32[1024,1024]{0,1:T(8,128)S(1)} fusion(bf16[4096,1024]{1,0:T(8,128)(2,1)} %copy-done.46, bf16[4096,1024]{1,0:T(8,128)(2,1)} %get-tuple-element.95), kind=kOutput, calls=%fused_computation.265 | convolution fusion | flops 8589934592 | bytes 20971520 | tf_op jit(solution)/shard_map/dot_general | solution.py:13
  254.1 8.2 copy.378
  262.4 13.3 %fusion.171 = f32[1024,1024]{0,1:T(8,128)S(1)} fusion(bf16[4096,1024]{1,0:T(8,128)(2,1)} %copy-done.43, bf16[4096,1024]{1,0:T(8,128)(2,1)} %copy-done.42), kind=kOutput, calls=%fused_computation.266 | convolution fusion | flops 8589934592 | bytes 20971520 | tf_op jit(solution)/shard_map/dot_general | solution.py:13
  280.9 8.1 copy.380
  289.1 12.8 %fusion.169 = f32[1024,1024]{0,1:T(8,128)S(1)} fusion(bf16[4096,1024]{1,0:T(8,128)(2,1)} %copy-done.41, bf16[4096,1024]{1,0:T(8,128)(2,1)} %param.7), kind=kOutput, calls=%fused_computation.264 | convolution fusion | flops 8589934592 | bytes 20971520 | tf_op jit(solution)/shard_map/dot_general | solution.py:13
  305.9 8.1 copy.376
  314.1 13.0 %convolution_bitcast_fusion = f32[1024,1024]{0,1:T(8,128)S(1)} fusion(bf16[4096,1024]{1,0:T(8,128)(2,1)} %get-tuple-element.99, bf16[4096,1024]{1,0:T(8,128)(2,1)} %param.8), kind=kOutput, calls=%fused_computation.126 | convolution fusion | flops 8589934592 | bytes 20971520 | tf_op jit(solution)/shard_map/dot_general | solution.py:13
  330.2 5.4 copy.382
  335.7 11.6 %fusion.156 = (f32[1,1024,1024]{2,1,0:T(8,128)}, f32[1,1024,1024]{2,1,0:T(8,128)S(1)}, f32[1,1024,1024]{2,1,0:T(8,128)}, f32[1,1024,1024]{2,1,0:T(8,128)}) fusion(f32[4,1024,1024]{2,1,0:T(8,128)} %param.10), kind=kLoop, calls=%fused_computation.250 | loop fusion | bytes 33554432 | tf_op jit(solution)/shard_map/slice | solution.py:106
  350.9 6.0 fusion.155
  361.7 75.4 %reduce-scatter.21.cloned.1.call-done = f32[32,3200]{1,0:T(8,128)} async-done(((f32[512,3200]{1,0:T(8,128)}), f32[32,3200]{1,0:T(8,128)}) %reduce-scatter.21.cloned.1.call-update) | async-done | bytes 409616 | tf_op jit(solution)/shard_map/reduce_scatter | solution.py:74
  437.1 75.9 %reduce-scatter.23.cloned.1.call-done = f32[32,3200]{1,0:T(8,128)} async-done(((f32[512,3200]{1,0:T(8,128)}), f32[32,3200]{1,0:T(8,128)}) %reduce-scatter.23.cloned.1.call-update) | async-done | bytes 409616 | tf_op jit(solution)/shard_map/reduce_scatter | solution.py:74
  513.0 75.9 %reduce-scatter.19.cloned.1.call-done = f32[32,3200]{1,0:T(8,128)} async-done(((f32[512,3200]{1,0:T(8,128)}), f32[32,3200]{1,0:T(8,128)}) %reduce-scatter.19.cloned.1.call-update) | async-done | bytes 409616 | tf_op jit(solution)/shard_map/reduce_scatter | solution.py:74
  596.4 57.3 %reduce-scatter.25.cloned.1.call-done = f32[32,2048]{1,0:T(8,128)} async-done(((f32[512,2048]{1,0:T(8,128)}), f32[32,2048]{1,0:T(8,128)}) %reduce-scatter.25.cloned.1.call-update) | async-done | bytes 262160
  655.2 6.5 fusion.104
  662.5 6.5 fusion.98
  669.8 6.7 fusion.101
  678.1 6.5 fusion.95
  687.6 24.1 %all_to_all.5 = f32[16,1,16384]{2,1,0:T(1,128)S(1)} all-to-all(f32[16,1,16384]{2,1,0:T(1,128)S(1)} %reshape.52), channel_id=1, replica_groups=mesh['data'=16] {'data'}, dimensions={0} | all-to-all | bytes 2097152 | tf_op jit(solution)/shard_map/all_to_all | solution.py:134
  731.7 5.3 fusion.110
  738.8 6.1 fusion.158
  756.4 9.3 %bitcast_select_fusion.7 = (f32[512,512]{1,0:T(8,128)}, f32[512,512]{1,0:T(8,128)}, f32[512,512]{1,0:T(8,128)}, f32[512,512]{1,0:T(8,128)}, f32[512,512]{1,0:T(8...) fusion(f32[512,512]{0,1:T(8,128)S(1)} %copy-done.10, ...), kind=kLoop, calls=%fused_computation.161 | loop fusion | flops 2621440 | bytes 26223616 | tf_op jit(solution)/shard_map/jit(_where)/select_n | solution.py:54
  781.3 10.1 %fusion.157 = (f32[512,512]{1,0:T(8,128)S(1)}, f32[512,512]{1,0:T(8,128)}, f32[512,512]{1,0:T(8,128)}, f32[512,512]{1,0:T(8,128)}, f32[512,512]{1,0:T(8,128)S(1)...) fusion(f32[512,5760]{1,0:T(8,128)} %all-gather.6.cloned.1.call-done), kind=kLoop, calls=%fused_computation.251 | loop fusion | bytes 29360128 | tf_op jit(solution)/shard_map/slice | solution.py:51
  827.7 10.0 %bitcast_select_fusion.1 = (f32[512,512]{1,0:T(8,128)}, f32[512,512]{1,0:T(8,128)}, f32[512,512]{1,0:T(8,128)}, f32[512,512]{1,0:T(8,128)}, f32[512,512]{1,0:T(8...) fusion(f32[512,512]{0,1:T(8,128)} %copy.412, ...), kind=kLoop, calls=%fused_computation.155 | loop fusion | flops 2883584 | bytes 26223616 | tf_op jit(solution)/shard_map/jit(_where)/select_n | solution.py:54
  868.7 8.2 pad_maximum_fusion.1
  876.9 6.3 pad_maximum_fusion
  883.2 12.0 %copy.418 = f32[4,1024,1024]{2,1,0:T(8,128)} copy(f32[4,1024,1024]{2,1,0:T(8,128)} %all-gather.4.cloned.1.call-done) | data formatting | bytes 33554432
  (251 shorter events, 182.4 us)
Async XLA Ops:
  7.2 353.4 %reduce-scatter.27.cloned.1.call-start = ((), (), s32[]{:S(2)}) async-start(), calls=%async_computation.14 | async-start | bytes 5013504 | tf_op jit(solution)/shard_map/reduce_scatter | solution.py:74
  8.4 6.9 copy-start.40
  21.2 18.1 %slice-start.4 = ((s8[8388608]{0:T(1024)(128)(4,1)}), s8[4194304]{0:T(1024)(128)(4,1)S(1)}, s32[]{:S(2)}) async-start(s8[8388608]{0:T(1024)(128)(4,1)} %bitcast.232), calls=%async_computation.20 | async-start | bytes 8388608
  28.2 11.1 %slice-start.5 = ((s8[8388608]{0:T(1024)(128)(4,1)}), s8[4194304]{0:T(1024)(128)(4,1)S(1)}, s32[]{:S(2)}) async-start(s8[8388608]{0:T(1024)(128)(4,1)} %bitcast.232), calls=%async_computation.21 | async-start | bytes 8388608
  52.6 7.0 copy-start.45
  82.7 21.4 %slice-start.6 = ((s8[8388608]{0:T(1024)(128)(4,1)}), s8[4194304]{0:T(1024)(128)(4,1)S(1)}, s32[]{:S(2)}) async-start(s8[8388608]{0:T(1024)(128)(4,1)} %bitcast.234), calls=%async_computation.22 | async-start | bytes 8388608
  88.5 15.5 %slice-start.7 = ((s8[8388608]{0:T(1024)(128)(4,1)}), s8[4194304]{0:T(1024)(128)(4,1)S(1)}, s32[]{:S(2)}) async-start(s8[8388608]{0:T(1024)(128)(4,1)} %bitcast.234), calls=%async_computation.23 | async-start | bytes 8388608
  120.2 17.3 %copy-start.43 = (bf16[4096,1024]{1,0:T(8,128)(2,1)}, bf16[4096,1024]{1,0:T(8,128)(2,1)S(1)}, u32[]{:S(2)}) copy-start(bf16[4096,1024]{1,0:T(8,128)(2,1)S(1)} %fusion.25) | copy-start | bytes 25165828
  144.3 10.7 %copy-start.44 = (bf16[4096,1024]{1,0:T(8,128)(2,1)S(1)}, bf16[4096,1024]{1,0:T(8,128)(2,1)}, u32[]{:S(2)}) copy-start(bf16[4096,1024]{1,0:T(8,128)(2,1)} %copy-done.43) | copy-start | bytes 25165828
  180.5 4.6 copy-start.41
  180.5 10.5 %slice-start.8 = ((s8[8388608]{0:T(1024)(128)(4,1)}), s8[4194304]{0:T(1024)(128)(4,1)S(1)}, s32[]{:S(2)}) async-start(s8[8388608]{0:T(1024)(128)(4,1)} %bitcast.236), calls=%async_computation.24 | async-start | bytes 8388608
  185.1 5.9 slice-start.9
  194.4 6.3 copy-start.27
  194.4 6.3 copy-start.28
  194.4 6.4 copy-start.34
  194.4 6.4 copy-start.36
  194.4 6.4 copy-start.38
  222.4 139.4 %reduce-scatter.29.cloned.1.call-start = ((), (), s32[]{:S(2)}) async-start(), calls=%async_computation.15 | async-start | bytes 7520256 | tf_op jit(solution)/shard_map/reduce_scatter | solution.py:74
  235.6 201.5 %reduce-scatter.21.cloned.1.call-start = ((), (), s32[]{:S(2)}) async-start(), calls=%async_computation.11 | async-start | bytes 6963200 | tf_op jit(solution)/shard_map/reduce_scatter | solution.py:74
  262.3 250.6 %reduce-scatter.23.cloned.1.call-start = ((), (), s32[]{:S(2)}) async-start(), calls=%async_computation.12 | async-start | bytes 6963200 | tf_op jit(solution)/shard_map/reduce_scatter | solution.py:74
  289.1 299.8 %reduce-scatter.19.cloned.1.call-start = ((), (), s32[]{:S(2)}) async-start(), calls=%async_computation.10 | async-start | bytes 6963200 | tf_op jit(solution)/shard_map/reduce_scatter | solution.py:74
  314.1 339.7 %reduce-scatter.25.cloned.1.call-start = ((), (), s32[]{:S(2)}) async-start(), calls=%async_computation.13 | async-start | bytes 4456448
  335.6 403.2 %all-gather.8.cloned.1.call-start = ((), (), s32[]{:S(2)}) async-start(), calls=%async_computation.9 | async-start | bytes 7520256 | tf_op jit(solution)/shard_map/all_gather | solution.py:77
  335.7 15.1 %slice-start = ((s8[16777216]{0:T(1024)(128)(4,1)}), s8[4194304]{0:T(1024)(128)(4,1)S(1)}, s32[]{:S(2)}) async-start(s8[16777216]{0:T(1024)(128)(4,1)} %bitcast.221), calls=%async_computation.16 | async-start | bytes 8388608
  335.7 15.0 %slice-start.1 = ((s8[16777216]{0:T(1024)(128)(4,1)}), s8[4194304]{0:T(1024)(128)(4,1)S(1)}, s32[]{:S(2)}) async-start(s8[16777216]{0:T(1024)(128)(4,1)} %bitcast.221), calls=%async_computation.17 | async-start | bytes 8388608
  335.7 15.0 %slice-start.2 = ((s8[16777216]{0:T(1024)(128)(4,1)}), s8[4194304]{0:T(1024)(128)(4,1)S(1)}, s32[]{:S(2)}) async-start(s8[16777216]{0:T(1024)(128)(4,1)} %bitcast.221), calls=%async_computation.18 | async-start | bytes 8388608
  335.7 15.2 %slice-start.3 = ((s8[16777216]{0:T(1024)(128)(4,1)}), s8[4194304]{0:T(1024)(128)(4,1)S(1)}, s32[]{:S(2)}) async-start(s8[16777216]{0:T(1024)(128)(4,1)} %bitcast.221), calls=%async_computation.19 | async-start | bytes 8388608
  360.6 234.3 %copy-start.33 = (f32[32,2304]{1,0:T(8,128)S(1)}, f32[32,2304]{1,0:T(8,128)}, u32[]{:S(2)}) copy-start(f32[32,2304]{1,0:T(8,128)} %reduce-scatter.27.cloned.1.call-done) | copy-start | bytes 884740
  361.7 233.0 %copy-start.29 = (f32[32,3456]{1,0:T(8,128)S(1)}, f32[32,3456]{1,0:T(8,128)}, u32[]{:S(2)}) copy-start(f32[32,3456]{1,0:T(8,128)} %reduce-scatter.29.cloned.1.call-done) | copy-start | bytes 1327108
  591.0 190.4 %all-gather.6.cloned.1.call-start = ((), (), s32[]{:S(2)}) async-start(), calls=%async_computation.8 | async-start | bytes 12533760 | tf_op jit(solution)/shard_map/all_gather | solution.py:77
  596.0 287.2 %all-gather.4.cloned.1.call-start = ((), (), s32[]{:S(2)}) async-start(), calls=%async_computation.7 | async-start | bytes 17825792 | tf_op jit(solution)/shard_map/all_gather | solution.py:137
  654.8 7.3 copy-start.30
  662.1 7.3 copy-start.31
  669.4 8.2 copy-start.32
  731.6 6.4 copy-start.35
  731.6 6.4 copy-start.37
  731.6 6.4 copy-start.39
  765.8 5.3 copy-start.22
  771.1 4.2 copy-start.9
  771.1 4.2 copy-start.20
  771.1 4.2 copy-start.21
  771.1 4.2 copy-start.25
  775.3 3.7 copy-start.23
  795.0 28.2 %copy-start.6 = (f32[512,512]{0,1:T(8,128)}, f32[512,512]{0,1:T(8,128)S(1)}, u32[]{:S(2)}) copy-start(f32[512,512]{0,1:T(8,128)S(1)} %copy.396) | copy-start | bytes 3145732
  859.7 7.5 copy-start.2
  862.2 5.0 copy-start
  862.2 6.5 copy-start.1
  868.7 8.2 copy-start.3
  (18 other events, 42.6 us)
Sparse Core Ops, SparseCore 0:
  222.5 63.2 reduce-scatter.26
  290.2 70.2 reduce-scatter.28
  362.8 74.2 reduce-scatter.20
  439.8 73.1 reduce-scatter.22
  515.7 73.1 reduce-scatter.18
  591.0 62.7 reduce-scatter.24
  656.6 53.7 all-gather.7
  712.6 60.9 all-gather.5
  775.9 76.2 all-gather.3
